TPU v7x, 256 devices: a whole 4x4x8 slice. The times are simulated.
256 devices in a mesh: section: 2 (over x_hi), feat: 16 (over y, x_lo, core), width: 8 (over z).
Axes of the slice: x: 4 (x_hi: 2, x_lo: 2; x = x_hi * 2 + x_lo), y: 4, z: 8, core: 2. Of those that a mesh axis runs over, the one named last changes fastest.
Arguments:
- mlp_inputs: bfloat16 [4, 1024, 2304], P('section', 'width'), may hold values from -6 to 6
- encoder: bfloat16 [4, 2304, 16384], P('section', 'width', 'feat'), may hold values from -0.125 to 0.125
- enc_bias: float32 [4, 16384], P('section', 'feat'), may hold values from -3 to 3
- decoder: bfloat16 [10, 16384, 2304], P('section', 'feat', 'width'), may hold values from -0.046875 to 0.046875
- dec_bias: float32 [4, 2304], P(None, 'width'), may hold values from -3 to 3
- targets: bfloat16 [4, 1024, 2304], P(None, None, 'width'), may hold values from -6 to 6
- live_rows: int32 [1024], replicated, may hold values 0 or 1
Outputs:
- errors: bfloat16 [4, 1024, 2304], P(None, None, 'width')
- gradients: bfloat16 [10, 16384, 2304], P('section', 'feat', 'width')
All inputs are finite; a program needn't handle non-finite values.
Results may differ from a plain program's by a relative error of at most 0.0042.
Values may be sent and summed in bfloat16 or wider, within the bound.
No kernel may reach another device: no remote copies, remote signals or barrier semaphores. Data moves between devices by JAX's collectives and lax.ppermute only.
A program may use at most 128 MiB of HBM per device.

v0:
```python
import jax
import jax.numpy as jnp
from jax import lax
from jax.sharding import PartitionSpec as P


def from_behind(value, axis, steps):
    count = lax.axis_size(axis)
    initial, last = (max(0, -steps), min(count, count - steps))
    return lax.ppermute(value, axis, [(source, source + steps) for source in range(initial, last)])


def pair_tables(layer_count):
    source_ids = []
    target_ids = []
    for source in range(layer_count):
        for target in range(source, layer_count):
            source_ids.append(source)
            target_ids.append(target)
    return (jnp.array(source_ids, jnp.int32), jnp.array(target_ids, jnp.int32))


def local(mlp_inputs, encoder, enc_bias, decoder, dec_bias, targets, live_rows):
    layers_here, tok_local, model_width = mlp_inputs.shape
    pre_act = jnp.einsum(
        "ltd,ldf->tlf",
        mlp_inputs,
        lax.all_gather(encoder, "width", axis=1, tiled=True),
        preferred_element_type=jnp.float32,
    )
    local_feats = jnp.maximum(pre_act + enc_bias[None, :, :], 0.0).astype(jnp.bfloat16)
    token_feats = lax.all_gather(local_feats, "width", axis=0, tiled=True)
    layers_all = dec_bias.shape[0]
    tokens_all = live_rows.shape[0]
    per_section = decoder.shape[0]
    source_ids, target_ids = pair_tables(layers_all)
    section_id = lax.axis_index("section")
    earlier = from_behind(token_feats[:, layers_here - 1], "section", 1)
    features = jnp.concatenate([earlier[:, None, :], token_feats], axis=1)
    first_layer = section_id * layers_here - 1
    rebuilt = jnp.zeros((layers_all, tokens_all, decoder.shape[2]), jnp.float32)
    chosen = []
    for pair_slot in range(per_section):
        pair_id = section_id * per_section + pair_slot
        source = source_ids[pair_id]
        target = target_ids[pair_id]
        picked = lax.dynamic_index_in_dim(features, source - first_layer, 1, keepdims=False)
        chosen.append((picked, target))
        partial_value = jnp.dot(picked, decoder[pair_slot], preferred_element_type=jnp.float32)
        current = lax.dynamic_index_in_dim(rebuilt, target, 0, keepdims=False)
        rebuilt = lax.dynamic_update_index_in_dim(rebuilt, current + partial_value, target, 0)
    summed = lax.psum(rebuilt, ("section", "feat"))
    keep_rows = live_rows.astype(jnp.float32)[None, :, None]
    errors = ((summed + dec_bias[:, None, :] - targets.astype(jnp.float32)) * keep_rows).astype(
        jnp.bfloat16
    )
    gradients = []
    for picked, target in chosen:
        residual = lax.dynamic_index_in_dim(errors, target, 0, keepdims=False)
        product = lax.dot_general(
            picked, residual, (((0,), (0,)), ((), ())), preferred_element_type=jnp.float32
        )
        gradients.append((product / tokens_all).astype(jnp.bfloat16))
    return (errors, jnp.stack(gradients))


def solution(mesh):
    placed = (
        P("section", "width", None),
        P("section", "width", "feat"),
        P("section", "feat"),
        P("section", "feat", "width"),
        P(None, "width"),
        P(None, None, "width"),
        P(),
    )
    return jax.shard_map(
        local,
        mesh=mesh,
        in_specs=placed,
        out_specs=(P(None, None, "width"), P("section", "feat", "width")),
        check_vma=False,
    )
```

profile of v0, /device:TPU:1, one launch (start us, length us, event | category | flops | bytes accessed | tf_op | source)
XLA Modules:
  0.0 397.8 jit_solution(8431505922366384273)
XLA Ops:
  7.2 0.0 copy-start
  7.2 0.0 all-gather.3.cloned.1.call-start
  7.2 0.7 all-gather.3.cloned.1.call-update
  7.9 0.0 all-gather.5.cloned.1.call-start
  8.0 109.4 %all-gather.3.cloned.1.call-done = bf16[2,2304,1024]{2,1,0:T(8,128)(2,1)} async-done(((bf16[2,288,1024]{2,1,0:T(8,128)(2,1)}), bf16[2,2304,1024]{2,1,0:T(8,128)(2,1)}) %all-gather.3.cloned.1.call-update) | async-done | bytes 9437200 | tf_op jit(solution)/shard_map/all_gather | solution.py:28
  117.3 0.0 copy-done
  117.3 7.3 %fusion.36 = bf16[128,2,1024]{0,2,1:T(8,128)(2,1)} fusion(bf16[2,2304,1024]{2,1,0:T(8,128)(2,1)} %all-gather.3.cloned.1.call-done, bf16[2,128,2304]{2,1,0:T(8,128)(2,1)S(1)} %copy-done, f32[2,1024]{1,0:T(2,128)} %param.11), kind=kOutput, calls=%fused_computation.59 | convolution fusion | flops 1208745984 | bytes 11149312 | tf_op jit(solution)/shard_map/ltd,ldf->tlf/dot_general | solution.py:25
  124.7 0.0 copy-start.5
  124.7 0.0 copy-start.6
  124.7 0.0 all-gather.5.cloned.1.call-update
  124.7 0.0 all-reduce.2.cloned.1.call-start
  124.7 57.6 %all-gather.5.cloned.1.call-done = bf16[1024,2,1024]{0,2,1:T(8,128)(2,1)} async-done(((bf16[128,2,1024]{0,2,1:T(8,128)(2,1)}), bf16[1024,2,1024]{0,2,1:T(8,128)(2,1)}) %all-gather.5.cloned.1.call-update) | async-done | bytes 4194320 | tf_op jit(solution)/shard_map/all_gather | solution.py:32
  182.4 3.1 slice_bitcast_fusion
  185.4 4.4 %collective-permute-start = (bf16[1024,1024]{0,1:T(8,128)(2,1)}, bf16[1024,1024]{0,1:T(8,128)(2,1)S(1)}, u32[]{:S(2)}, u32[]{:S(2)}) collective-permute-start(bf16[1024,1024]{0,1:T(8,128)(2,1)} %slice_bitcast_fusion), channel_id=1, source_target_pairs={{0,128},{1,129},{2,130},{3,131},{4,132},{5,133},{6,134},{7,135},{8... | collective-permute-start | bytes 6291464 | tf_op jit(solution)/shard_map/ppermute | solution.py:10
  189.9 0.0 copy-done.5
  189.9 0.0 copy-done.6
  189.9 0.7 fusion.72
  203.2 26.7 %collective-permute-done = bf16[1024,1024]{0,1:T(8,128)(2,1)S(1)} collective-permute-done((bf16[1024,1024]{0,1:T(8,128)(2,1)}, bf16[1024,1024]{0,1:T(8,128)(2,1)S(1)}, u32[]{:S(2)}, u32[]{:S(2)}) %collective-permute-start) | collective-permute-done | bytes 2097184 | tf_op jit(solution)/shard_map/ppermute | solution.py:10
  229.9 0.0 copy-start.1
  229.9 3.0 broadcast_in_dim.25
  232.9 0.8 copy-done.1
  233.7 0.0 copy-start.3
  233.7 3.4 fusion.18
  237.1 1.3 constant_dynamic-slice_fusion.3
  238.5 0.0 copy-done.3
  238.5 2.2 fusion.17
  240.7 1.3 constant_dynamic-slice_fusion.2
  242.1 2.2 fusion.15
  244.3 1.3 constant_dynamic-slice_fusion.1
  245.6 2.3 fusion.13
  247.9 1.3 constant_dynamic-slice_fusion
  249.3 2.2 fusion.11
  251.5 0.0 copy-start.8
  251.5 0.0 copy-start.7
  251.5 0.0 all-reduce.2.cloned.1.call-update
  251.5 0.7 copy-done.8
  252.2 126.4 %all-reduce.2.cloned.1.call-done = f32[4,1024,288]{1,2,0:T(8,128)} async-done(((f32[4,1024,288]{1,2,0:T(8,128)}), f32[4,1024,288]{1,2,0:T(8,128)}) %all-reduce.2.cloned.1.call-update) | async-done | bytes 4718608 | tf_op jit(solution)/shard_map/psum | solution.py:52
  378.6 0.0 copy-done.7
  378.6 3.9 multiply_convert_fusion
  382.5 0.3 copy-done.2
  382.8 1.4 fusion.35
  384.2 1.4 fusion.33
  385.6 1.4 fusion.31
  386.9 1.4 fusion.29
  388.3 0.0 copy-done.4
  388.3 1.4 fusion.27
  389.7 0.0 copy-start.9
  389.7 1.6 copy-done.9
  (3 shorter events, 0.0 us)
Async XLA Ops:
  7.2 110.2 %copy-start = (bf16[2,128,2304]{2,1,0:T(8,128)(2,1)S(1)}, bf16[2,128,2304]{2,1,0:T(8,128)(2,1)}, u32[]{:S(2)}) copy-start(bf16[2,128,2304]{2,1,0:T(8,128)(2,1)} %param.9) | copy-start | bytes 3538948
  7.2 110.2 %all-gather.3.cloned.1.call-start = ((), (), s32[]{:S(2)}) async-start(), calls=%async_computation | async-start | bytes 10616832 | tf_op jit(solution)/shard_map/all_gather | solution.py:28
  7.9 174.4 %all-gather.5.cloned.1.call-start = ((), (), s32[]{:S(2)}) async-start(), calls=%async_computation.1 | async-start | bytes 4718592 | tf_op jit(solution)/shard_map/all_gather | solution.py:32
  124.7 65.2 %copy-start.5 = (s32[10]{0:T(128)S(1)}, s32[10]{0:T(128)}, u32[]{:S(2)}) copy-start(s32[10]{0:T(128)} %constant.92.clone) | copy-start | bytes 124
  124.7 65.2 %copy-start.6 = (s32[10]{0:T(128)S(1)}, s32[10]{0:T(128)}, u32[]{:S(2)}) copy-start(s32[10]{0:T(128)} %constant.93.clone) | copy-start | bytes 124
  124.7 253.9 %all-reduce.2.cloned.1.call-start = ((), (), s32[]{:S(2)}) async-start(), calls=%async_computation.2 | async-start | bytes 9437184 | tf_op jit(solution)/shard_map/psum | solution.py:52
  185.4 44.5 %collective-permute-start = (bf16[1024,1024]{0,1:T(8,128)(2,1)}, bf16[1024,1024]{0,1:T(8,128)(2,1)S(1)}, u32[]{:S(2)}, u32[]{:S(2)}) collective-permute-start(bf16[1024,1024]{0,1:T(8,128)(2,1)} %slice_bitcast_fusion), channel_id=1, source_target_pairs={{0,128},{1,129},{2,130},{3,131},{4,132},{5,133},{6,134},{7,135},{8... | collective-permute-start | bytes 6291464 | tf_op jit(solution)/shard_map/ppermute | solution.py:10
  229.9 3.8 copy-start.1
  233.7 4.7 %copy-start.3 = (bf16[5,1024,288]{1,2,0:T(8,128)(2,1)S(1)}, bf16[5,1024,288]{1,2,0:T(8,128)(2,1)}, u32[]{:S(2)}) copy-start(bf16[5,1024,288]{1,2,0:T(8,128)(2,1)} %param.12) | copy-start | bytes 8847364
  251.5 0.7 copy-start.8
  251.5 127.1 %copy-start.7 = (f32[4,288]{1,0:T(4,128)S(1)}, f32[4,288]{1,0:T(4,128)}, u32[]{:S(2)}) copy-start(f32[4,288]{1,0:T(4,128)} %param.13) | copy-start | bytes 13828
  378.6 4.2 %copy-start.2 = (bf16[1024,2,1024]{0,2,1:T(8,128)(2,1)S(1)}, bf16[1024,2,1024]{0,2,1:T(8,128)(2,1)}, u32[]{:S(2)}) copy-start(bf16[1024,2,1024]{0,2,1:T(8,128)(2,1)} %all-gather.5.cloned.1.call-done) | copy-start | bytes 12582916
  382.8 5.5 %copy-start.4 = (bf16[4,1024,288]{1,2,0:T(8,128)(2,1)}, bf16[4,1024,288]{1,2,0:T(8,128)(2,1)S(1)}, u32[]{:S(2)}) copy-start(bf16[4,1024,288]{1,2,0:T(8,128)(2,1)S(1)} %multiply_convert_fusion) | copy-start | bytes 7077892
  389.7 1.6 copy-start.9
Sparse Core Ops, SparseCore 0:
  9.8 107.5 all-gather.2
  124.8 57.5 all-gather.4
  251.6 126.9 all-reduce.1
where the time goes:
time: 398 us
  waiting for transfers between devices  321 us (81%)
  matrix products  26.5 us (7%)
  between operations  26.5 us (7%)
  local copies, waits for them, and re-layouts  15.5 us (4%)
  starting transfers between devices  4.52 us (1%)
    psum x1, waiting for transfers between devices, local(): summed = lax.psum(rebuilt, ('section', 'feat'))  126 us
    all_gather x1, waiting for transfers between devices, local(): lax.all_gather(encoder, 'width', axis=1, tiled=True)  109 us
    all_gather x1, waiting for transfers between devices, local(): token_feats = lax.all_gather(local_feats, 'width', axis=0, tiled=True)  57.6 us
    ppermute x1, waiting for transfers between devices, from_behind(): lax.ppermute(value, axis, [(source, source + steps) for source in range(i...  26.7 us
    dot_general x5, matrix products, local(): jnp.dot(picked, decoder[pair_slot], preferred_element_type=jnp.float32)  12.3 us
  transfers between devices with their start and end apart: 4, of which 4 were waited for; matrix products, arithmetic and copies ran while one was open for 0% of the time, Pallas kernels for 0%

commit v1 on v0

--- a/solution.py
+++ b/solution.py
@@ -49,7 +49,7 @@
         partial_value = jnp.dot(picked, decoder[pair_slot], preferred_element_type=jnp.float32)
         current = lax.dynamic_index_in_dim(rebuilt, target, 0, keepdims=False)
         rebuilt = lax.dynamic_update_index_in_dim(rebuilt, current + partial_value, target, 0)
-    summed = lax.psum(rebuilt, ("section", "feat"))
+    summed = lax.psum(lax.psum(rebuilt, "section"), "feat")
     keep_rows = live_rows.astype(jnp.float32)[None, :, None]
     errors = ((summed + dec_bias[:, None, :] - targets.astype(jnp.float32)) * keep_rows).astype(
         jnp.bfloat16

time: 398 us -> 553 us (1.39)
  waiting for transfers between devices: 321 us -> 475 us
    psum x1 -> x2, waiting for transfers between devices: 126 us -> 281 us  [local(): summed = lax.psum(lax.psum(rebuilt, 'section'), 'feat')]
  transfers between devices with their start and end apart: 4 -> 5, of which waited for: 4 -> 5; matrix products, arithmetic and copies ran while one was open for 0% -> 0% of each run, Pallas kernels for 0% -> 0%
where the time goes in v1:
time: 553 us; the launch traced here: 552 us
  waiting for transfers between devices  475 us (86%)
  matrix products  26.5 us (5%)
  between operations  26.5 us (5%)
  local copies, waits for them, and re-layouts  15.5 us (3%)
    psum x2, waiting for transfers between devices, local(): summed = lax.psum(lax.psum(rebuilt, 'section'), 'feat')  281 us
    all_gather x1, waiting for transfers between devices, local(): lax.all_gather(encoder, 'width', axis=1, tiled=True)  109 us
    all_gather x1, waiting for transfers between devices, local(): token_feats = lax.all_gather(local_feats, 'width', axis=0, tiled=True)  57.6 us
    ppermute x1, waiting for transfers between devices, from_behind(): lax.ppermute(value, axis, [(source, source + steps) for source in range(i...  26.9 us
    dot_general x5, matrix products, local(): jnp.dot(picked, decoder[pair_slot], preferred_element_type=jnp.float32)  12.3 us
  transfers between devices with their start and end apart: 5, of which 5 were waited for; matrix products, arithmetic and copies ran while one was open for 0% of the time, Pallas kernels for 0%

profile of v1, /device:TPU:1, one launch (start us, length us, event | category | flops | bytes accessed | tf_op | source)
XLA Modules:
  0.0 552.2 jit_solution(10342985006708061985)
XLA Ops:
  7.2 0.0 copy-start
  7.2 0.0 all-gather.3.cloned.1.call-start
  7.2 0.7 all-gather.3.cloned.1.call-update
  7.9 0.0 all-gather.5.cloned.1.call-start
  8.0 109.4 %all-gather.3.cloned.1.call-done = bf16[2,2304,1024]{2,1,0:T(8,128)(2,1)} async-done(((bf16[2,288,1024]{2,1,0:T(8,128)(2,1)}), bf16[2,2304,1024]{2,1,0:T(8,128)(2,1)}) %all-gather.3.cloned.1.call-update) | async-done | bytes 9437200 | tf_op jit(solution)/shard_map/all_gather | solution.py:28
  117.3 0.0 copy-done
  117.3 7.3 %fusion.36 = bf16[128,2,1024]{0,2,1:T(8,128)(2,1)} fusion(bf16[2,2304,1024]{2,1,0:T(8,128)(2,1)} %all-gather.3.cloned.1.call-done, bf16[2,128,2304]{2,1,0:T(8,128)(2,1)S(1)} %copy-done, f32[2,1024]{1,0:T(2,128)} %param.11), kind=kOutput, calls=%fused_computation.59 | convolution fusion | flops 1208745984 | bytes 11149312 | tf_op jit(solution)/shard_map/ltd,ldf->tlf/dot_general | solution.py:25
  124.7 0.0 copy-start.5
  124.7 0.0 copy-start.6
  124.7 0.0 all-gather.5.cloned.1.call-update
  124.7 0.0 all-reduce.3.cloned.1.call-start
  124.7 57.6 %all-gather.5.cloned.1.call-done = bf16[1024,2,1024]{0,2,1:T(8,128)(2,1)} async-done(((bf16[128,2,1024]{0,2,1:T(8,128)(2,1)}), bf16[1024,2,1024]{0,2,1:T(8,128)(2,1)}) %all-gather.5.cloned.1.call-update) | async-done | bytes 4194320 | tf_op jit(solution)/shard_map/all_gather | solution.py:32
  182.4 3.1 slice_bitcast_fusion
  185.4 4.2 collective-permute-start
  189.7 0.0 copy-done.5
  189.7 0.0 copy-done.6
  189.7 0.7 fusion.72
  203.0 26.9 %collective-permute-done = bf16[1024,1024]{0,1:T(8,128)(2,1)S(1)} collective-permute-done((bf16[1024,1024]{0,1:T(8,128)(2,1)}, bf16[1024,1024]{0,1:T(8,128)(2,1)S(1)}, u32[]{:S(2)}, u32[]{:S(2)}) %collective-permute-start) | collective-permute-done | bytes 2097184 | tf_op jit(solution)/shard_map/ppermute | solution.py:10
  229.9 0.0 copy-start.1
  229.9 3.0 broadcast_in_dim.25
  232.9 0.8 copy-done.1
  233.7 3.4 fusion.18
  237.1 1.3 constant_dynamic-slice_fusion.3
  238.5 0.0 copy-done.3
  238.5 2.2 fusion.17
  240.7 1.3 constant_dynamic-slice_fusion.2
  242.1 2.2 fusion.15
  244.3 1.3 constant_dynamic-slice_fusion.1
  245.6 2.3 fusion.13
  247.9 1.3 constant_dynamic-slice_fusion
  249.3 2.2 fusion.11
  251.5 0.0 all-reduce.3.cloned.1.call-update
  251.5 0.2 all-reduce.5.cloned.1.call-start
  251.7 136.4 %all-reduce.3.cloned.1.call-done = f32[4,1024,288]{1,2,0:T(8,128)} async-done(((f32[4,1024,288]{1,2,0:T(8,128)}), f32[4,1024,288]{1,2,0:T(8,128)}) %all-reduce.3.cloned.1.call-update) | async-done | bytes 4718608 | tf_op jit(solution)/shard_map/psum | solution.py:52
  388.2 0.0 all-reduce.5.cloned.1.call-update
  388.2 0.7 copy-done.8
  388.9 144.1 %all-reduce.5.cloned.1.call-done = f32[4,1024,288]{1,2,0:T(8,128)} async-done(((f32[4,1024,288]{1,2,0:T(8,128)}), f32[4,1024,288]{1,2,0:T(8,128)}) %all-reduce.5.cloned.1.call-update) | async-done | bytes 4718608 | tf_op jit(solution)/shard_map/psum | solution.py:52
  533.0 0.0 copy-done.7
  533.0 3.9 multiply_convert_fusion
  536.9 0.3 copy-done.2
  537.2 1.4 fusion.35
  538.6 1.4 fusion.33
  540.0 1.4 fusion.31
  541.3 1.4 fusion.29
  542.7 0.0 copy-done.4
  542.7 1.4 fusion.27
  544.1 0.0 copy-start.9
  544.1 1.6 copy-done.9
  (6 shorter events, 0.0 us)
Async XLA Ops:
  7.2 110.2 %copy-start = (bf16[2,128,2304]{2,1,0:T(8,128)(2,1)S(1)}, bf16[2,128,2304]{2,1,0:T(8,128)(2,1)}, u32[]{:S(2)}) copy-start(bf16[2,128,2304]{2,1,0:T(8,128)(2,1)} %param.9) | copy-start | bytes 3538948
  7.2 110.2 %all-gather.3.cloned.1.call-start = ((), (), s32[]{:S(2)}) async-start(), calls=%async_computation | async-start | bytes 10616832 | tf_op jit(solution)/shard_map/all_gather | solution.py:28
  7.9 174.4 %all-gather.5.cloned.1.call-start = ((), (), s32[]{:S(2)}) async-start(), calls=%async_computation.1 | async-start | bytes 4718592 | tf_op jit(solution)/shard_map/all_gather | solution.py:32
  124.7 65.0 %copy-start.5 = (s32[10]{0:T(128)S(1)}, s32[10]{0:T(128)}, u32[]{:S(2)}) copy-start(s32[10]{0:T(128)} %constant.92.clone) | copy-start | bytes 124
  124.7 65.0 %copy-start.6 = (s32[10]{0:T(128)S(1)}, s32[10]{0:T(128)}, u32[]{:S(2)}) copy-start(s32[10]{0:T(128)} %constant.93.clone) | copy-start | bytes 124
  124.7 263.5 %all-reduce.3.cloned.1.call-start = ((), (), s32[]{:S(2)}) async-start(), calls=%async_computation.2 | async-start | bytes 9437184 | tf_op jit(solution)/shard_map/psum | solution.py:52
  185.4 44.5 %collective-permute-start = (bf16[1024,1024]{0,1:T(8,128)(2,1)}, bf16[1024,1024]{0,1:T(8,128)(2,1)S(1)}, u32[]{:S(2)}, u32[]{:S(2)}) collective-permute-start(bf16[1024,1024]{0,1:T(8,128)(2,1)} %slice_bitcast_fusion), channel_id=1, source_target_pairs={{0,128},{1,129},{2,130},{3,131},{4,132},{5,133},{6,134},{7,135},{8... | collective-permute-start | bytes 6291464 | tf_op jit(solution)/shard_map/ppermute | solution.py:10
  229.9 3.8 copy-start.1
  233.7 4.7 copy-start.3
  251.5 281.5 %all-reduce.5.cloned.1.call-start = ((), (), s32[]{:S(2)}) async-start(), calls=%async_computation.3 | async-start | bytes 9437184 | tf_op jit(solution)/shard_map/psum | solution.py:52
  388.2 0.7 copy-start.8
  388.2 144.8 %copy-start.7 = (f32[4,288]{1,0:T(4,128)S(1)}, f32[4,288]{1,0:T(4,128)}, u32[]{:S(2)}) copy-start(f32[4,288]{1,0:T(4,128)} %param.13) | copy-start | bytes 13828
  533.0 4.2 copy-start.2
  537.2 5.5 copy-start.4
  544.1 1.6 copy-start.9
Sparse Core Ops, SparseCore 0:
  9.8 107.5 all-gather.2
  124.8 57.5 all-gather.4
  251.6 136.5 all-reduce.2
  390.7 142.2 all-reduce.4
